TPU v7x, 256 devices: a whole 4x4x8 slice. The times are simulated.
256 devices in a mesh: dp: 128 (over y, x_lo, z, core), rep: 2 (over x_hi).
Axes of the slice: x: 4 (x_hi: 2, x_lo: 2; x = x_hi * 2 + x_lo), y: 4, z: 8, core: 2. Of those that a mesh axis runs over, the one named last changes fastest.
Arguments:
- q_hidden: bfloat16 [2, 128, 128, 768], P('rep', 'dp'), may hold values from -8 to 8
- p_hidden: bfloat16 [2, 128, 128, 768], P('rep', 'dp'), may hold values from -8 to 8
- w_up: bfloat16 [1536, 768], replicated, may hold values from -0.21875 to 0.21875
- w_down: bfloat16 [1536, 768], replicated, may hold values from -0.15625 to 0.15625
- pos_index: int32 [2, 128], P('rep', 'dp'), may hold values from 0 to 127
- hard_index: int32 [2, 128, 2], P('rep', 'dp'), may hold values from 0 to 127
Outputs:
- w_up_grad: float32 [1536, 768], P(('dp', 'rep'))
- mean_loss: float32 [], replicated
All inputs are finite; a program needn't handle non-finite values.
Results may differ from a plain program's by a relative error of at most 0.008.
Values may be sent and summed in bfloat16 or wider, within the bound.
A program may use at most 64 MiB of HBM per device.

v0:
```python
import math

import jax
import jax.numpy as jnp
from jax import lax
from jax.sharding import Mesh
from jax.sharding import PartitionSpec as P

DP = ("dp_0", "dp_1", "dp_2", "dp_3")
DP_REP = ("dp_0", "dp_1", "dp_2", "dp_3", "rep")


norm_eps = 1e-06
HARD_BOOST = 1.5


def from_everyone(shard, axis):
    copies = jnp.broadcast_to(shard, (lax.axis_size(axis), *shard.shape))
    return lax.all_to_all(copies, axis, split_axis=0, concat_axis=0, tiled=True)


def joined_along(tiles, dim):
    dims = list(tiles.shape[1:])
    dims[dim] *= tiles.shape[0]
    return jnp.moveaxis(tiles, 0, dim).reshape(dims)


def gather_axes(shard, axes, dim):
    far, near = axes
    tiles = from_everyone(from_everyone(shard, far), near)
    return joined_along(tiles.swapaxes(0, 1).reshape(-1, *shard.shape), dim)


def sent_together(arrays, axis, dim, along):
    columns = [a.reshape(*a.shape[:along], -1) for a in arrays]
    both = jnp.concatenate(columns, axis=along)
    out, at, done = (lax.all_gather(both, axis, axis=dim, tiled=True), 0, [])
    for a, column in zip(arrays, columns):
        section = out[..., at : at + column.shape[along]]
        done.append(section.reshape(*section.shape[:along], *a.shape[along:]))
        at += column.shape[along]
    return tuple(done)


def one_axis_at_a_time(shard, axes):
    for axis in axes:
        shard = lax.psum(shard, axis)
    return shard


def in_blocks(shard, dim, count):
    before, after = (shard.shape[:dim], shard.shape[dim + 1 :])
    return jnp.moveaxis(shard.reshape(*before, count, -1, *after), dim, 0)


def own_tiles(shard, axis, dim):
    count = lax.axis_size(axis)
    tiles = in_blocks(shard, dim, count)
    length = shard.size // count
    spare = max(2048 - length, -length % 1024)
    padded = jnp.pad(tiles.reshape(count, length), ((0, 0), (0, spare)))
    own = lax.psum_scatter(padded.reshape(-1, 128), axis, scatter_dimension=0, tiled=True)
    return own.reshape(-1)[:length].reshape(tiles.shape[1:])


def gelu_slope(values):
    cdf_part = 0.5 * (1.0 + lax.erf(values * (1.0 / math.sqrt(2.0))))
    return cdf_part + values * jnp.exp(-0.5 * values * values) * (1.0 / math.sqrt(2.0 * math.pi))


def contract_rows(left, right):
    return lax.dot_general(
        left, right, (((0,), (0,)), ((), ())), preferred_element_type=jnp.float32
    )


def shards(q_hidden, p_hidden, w_up, w_down, pos_index, hard_index):
    pair_count = q_hidden.shape[1]
    length = q_hidden.shape[2]
    features = q_hidden.shape[3]
    pool_size = pair_count * lax.axis_size(DP)
    tokens = jnp.concatenate([q_hidden[0], p_hidden[0]], 0).reshape(-1, features)
    pre_act = lax.dot_general(
        tokens, w_up, (((1,), (1,)), ((), ())), preferred_element_type=jnp.float32
    )
    hidden = jax.nn.gelu(pre_act, approximate=False).astype(jnp.bfloat16)
    summed = tokens.astype(jnp.float32) + jnp.dot(
        hidden, w_down, preferred_element_type=jnp.float32
    )
    row_mean = jnp.mean(summed, -1, keepdims=True)
    centred = summed - row_mean
    inv_scale = lax.rsqrt(jnp.mean(centred * centred, -1, keepdims=True) + norm_eps)
    normed = centred * inv_scale
    embedded = jnp.mean(normed.reshape(2 * pair_count, length, features), 1).astype(jnp.bfloat16)
    query_embed = embedded[:pair_count]
    passage_embed = embedded[pair_count:]
    all_passages = gather_axes(passage_embed, (("dp_0", "dp_1", "dp_2"), "dp_3"), 0)
    columns = jnp.arange(pool_size, dtype=jnp.int32)
    all_queries = gather_axes(query_embed, (("dp_0", "dp_1", "dp_2"), "dp_3"), 0)
    all_targets, all_negatives = sent_together((pos_index[0], hard_index[0]), DP, 0, 1)
    scores = lax.dot_general(
        all_queries, all_passages, (((1,), (1,)), ((), ())), preferred_element_type=jnp.float32
    )
    hard_mask = jnp.any(all_negatives[:, :, None] == columns, axis=1)
    logits = scores + HARD_BOOST * hard_mask.astype(jnp.float32)
    row_max = jnp.max(logits, -1, keepdims=True)
    log_total = row_max + jnp.log(jnp.sum(jnp.exp(logits - row_max), -1, keepdims=True))
    target = all_targets[:, None] == columns
    picked = jnp.sum(jnp.where(target, logits, 0.0), -1)
    weights = (jnp.exp(logits - log_total) - target.astype(jnp.float32)).astype(jnp.bfloat16)
    losses, weights = (log_total[:, 0] - picked, weights)
    first_row = lax.axis_index(DP) * pair_count
    own_losses = lax.dynamic_slice_in_dim(losses, first_row, pair_count, 0)
    own_rows = lax.dynamic_slice_in_dim(weights, first_row, pair_count, 0)
    own_columns = lax.dynamic_slice_in_dim(weights, first_row, pair_count, 1)
    d_query = jnp.dot(own_rows, all_passages, preferred_element_type=jnp.float32)
    d_passage = contract_rows(own_columns, all_queries)
    loss_sum = one_axis_at_a_time(jnp.sum(own_losses), DP_REP)
    mean_loss = loss_sum / (pool_size * lax.axis_size("rep"))
    d_embed = jnp.concatenate([d_query, d_passage], 0)
    grad_out = jnp.repeat(d_embed / length, length, axis=0)
    grad_resid = inv_scale * (
        grad_out
        - jnp.mean(grad_out, -1, keepdims=True)
        - normed * jnp.mean(grad_out * normed, -1, keepdims=True)
    )
    grad_low = grad_resid.astype(jnp.bfloat16)
    grad_hidden = lax.dot_general(
        grad_low, w_down, (((1,), (1,)), ((), ())), preferred_element_type=jnp.float32
    )
    grad_pre = (grad_hidden * gelu_slope(pre_act)).astype(jnp.bfloat16)
    up_terms = contract_rows(grad_pre, tokens)
    w_up_grad = own_tiles(up_terms, DP_REP, 0)
    return (w_up_grad, mean_loss)


def solution(mesh):
    finer = Mesh(
        mesh.devices.reshape(4, 2, 8, 2, mesh.shape["rep"]), ("dp_0", "dp_1", "dp_2", "dp_3", "rep")
    )
    return jax.shard_map(
        shards,
        mesh=finer,
        in_specs=(
            P("rep", DP, None, None),
            P("rep", DP, None, None),
            P(),
            P(),
            P("rep", DP),
            P("rep", DP, None),
        ),
        out_specs=(P(DP_REP, None), P()),
        check_vma=False,
    )
```

profile of v0, /device:TPU:1, one launch (start us, length us, event | category | flops | bytes accessed | tf_op | source)
XLA Modules:
  0.0 538.9 jit_solution(12899937329911014059)
XLA Ops:
  7.2 1.2 pad_maximum_fusion
  8.4 2.5 fusion.100
  10.9 4.1 fusion.98
  15.8 0.8 broadcast_in_dim.14
  16.6 0.5 broadcast.114
  17.1 2.7 reduce.11
  19.8 1.6 reshape.93
  21.4 13.8 %all-to-all-start.2 = ((bf16[64,2,384]{2,1,0:T(2,128)(2,1)}), bf16[64,2,384]{2,1,0:T(2,128)(2,1)}, u32[]{:S(2)}, u32[]{:S(2)}) async-start(bf16[64,2,384]{2,1,0:T(2,128)(2,1)} %reshape.93), calls=%async_computation.2 | async-start | bytes 196608 | tf_op jit(solution)/shard_map/all_to_all | solution.py:19
  36.0 157.7 %all-gather = s32[128,1,3]{2,1,0:T(1,128)S(1)} all-gather(s32[1,1,3]{2,1,0:T(1,128)S(1)} %add_bitcast_fusion), channel_id=1, replica_groups=mesh['dp_0'=4,'dp_1'=2,'dp_2'=8,'dp_3'=2,'rep'=2] {'dp_0','dp_1','dp_2',..., dimensions={0}, use_global_device_ids=true | all-gather | bytes 1548 | tf_op jit(solution)/shard_map/all_gather | solution.py:37
  193.7 0.6 copy-done.2
  194.3 0.7 slice.29
  195.0 0.9 copy.12
  195.9 0.8 broadcast_in_dim.11
  196.7 2.7 reduce.10
  199.4 1.6 reshape.91
  201.0 1.6 reshape.94
  202.6 0.9 copy.18
  203.6 4.4 all_to_all.26
  208.0 5.4 %all-to-all-start = ((bf16[64,2,384]{2,1,0:T(2,128)(2,1)}), bf16[64,2,384]{2,1,0:T(2,128)(2,1)}, u32[]{:S(2)}, u32[]{:S(2)}) async-start(bf16[64,2,384]{2,1,0:T(2,128)(2,1)} %reshape.91), calls=%async_computation | async-start | bytes 196608 | tf_op jit(solution)/shard_map/all_to_all | solution.py:19
  213.7 1.5 slice_reduce_fusion
  215.1 1.8 copy.11
  216.9 1.7 reshape_reshape.10
  218.6 4.7 all-to-all-done
  223.3 1.6 reshape.92
  224.9 0.9 copy.19
  225.9 5.0 all_to_all.27
  230.9 0.9 copy.10
  231.8 1.7 reshape_reshape.9
  233.5 1.3 fusion.99
  234.7 0.7 select_reduce_fusion
  235.5 0.7 subtract_convert_fusion
  236.1 1.1 fusion.58
  237.4 1.1 fusion.56
  238.7 0.9 fusion.19
  239.7 1.0 fusion.18
  240.7 5.4 fusion.15
  246.0 5.5 %reshape_reshape.11 = f32[256,4608]{1,0:T(8,128)} reshape(f32[1536,768]{1,0:T(8,128)} %fusion.15) | data formatting | bytes 9437184 | tf_op jit(solution)/shard_map/reshape;reshape | solution.py:61
  251.6 5.3 pad.4
  256.8 6.3 %reshape.76 = f32[10240,128]{1,0:T(8,128)} reshape(f32[256,5120]{1,0:T(8,128)} %pad.4) | data formatting | bytes 10485760 | tf_op jit(solution)/shard_map/reshape | solution.py:62
  263.2 0.6 dynamic_slice.11
  263.8 7.1 %psum.35 = f32[]{:T(128)} all-reduce(f32[]{:T(128)} %bitcast.12), channel_id=1, replica_groups=mesh['dp_0'=4,'dp_1'=2,'dp_2'=8,'dp_3'=2,'rep'=2] {'dp_0'}, use_global_device_ids=true, to_apply=%region_10.11 | all-reduce | flops 1 | bytes 8 | tf_op jit(solution)/shard_map/psum | solution.py:47
  270.9 4.4 psum.36
  275.2 12.8 %psum.37 = f32[]{:T(128)} all-reduce(f32[]{:T(128)} %psum.36), channel_id=1, replica_groups=mesh['dp_0'=4,'dp_1'=2,'dp_2'=8,'dp_3'=2,'rep'=2] {'dp_2'}, use_global_device_ids=true, to_apply=%region_12.13 | all-reduce | flops 1 | bytes 8 | tf_op jit(solution)/shard_map/psum | solution.py:47
  288.1 9.0 %psum.38 = f32[]{:T(128)} all-reduce(f32[]{:T(128)} %psum.37), channel_id=1, replica_groups=mesh['dp_0'=4,'dp_1'=2,'dp_2'=8,'dp_3'=2,'rep'=2] {'dp_3'}, use_global_device_ids=true, to_apply=%region_13.14 | all-reduce | flops 1 | bytes 8 | tf_op jit(solution)/shard_map/psum | solution.py:47
  297.1 5.9 %psum.39 = f32[]{:T(128)} all-reduce(f32[]{:T(128)} %psum.38), channel_id=1, replica_groups=mesh['dp_0'=4,'dp_1'=2,'dp_2'=8,'dp_3'=2,'rep'=2] {'rep'}, use_global_device_ids=true, to_apply=%region_14.15 | all-reduce | flops 1 | bytes 8 | tf_op jit(solution)/shard_map/psum | solution.py:47
  303.6 226.0 %all-reduce.4.cloned.1.call-done = f32[10240,128]{1,0:T(8,128)} async-done(((f32[10240,128]{1,0:T(8,128)}), f32[10240,128]{1,0:T(8,128)}) %all-reduce.4.cloned.1.call-update) | async-done | bytes 5242896
  529.6 0.7 constant_dynamic-slice_fusion
  530.3 0.6 reshape.77
  (35 shorter events, 1.6 us)
Async XLA Ops:
  7.2 3.7 copy-start
  10.9 4.1 copy-start.1
  15.0 20.9 %copy-start.7 = (s32[1,1,2]{2,1,0:T(1,128)S(1)}, s32[1,1,2]{2,1,0:T(1,128)}, u32[]{:S(2)}) copy-start(s32[1,1,2]{2,1,0:T(1,128)} %param.11) | copy-start | bytes 28
  15.0 0.5 copy-start.3
  15.2 0.6 copy-start.5
  21.4 179.6 %all-to-all-start.2 = ((bf16[64,2,384]{2,1,0:T(2,128)(2,1)}), bf16[64,2,384]{2,1,0:T(2,128)(2,1)}, u32[]{:S(2)}, u32[]{:S(2)}) async-start(bf16[64,2,384]{2,1,0:T(2,128)(2,1)} %reshape.93), calls=%async_computation.2 | async-start | bytes 196608 | tf_op jit(solution)/shard_map/all_to_all | solution.py:19
  193.7 0.6 copy-start.2
  208.0 15.3 %all-to-all-start = ((bf16[64,2,384]{2,1,0:T(2,128)(2,1)}), bf16[64,2,384]{2,1,0:T(2,128)(2,1)}, u32[]{:S(2)}, u32[]{:S(2)}) async-start(bf16[64,2,384]{2,1,0:T(2,128)(2,1)} %reshape.91), calls=%async_computation | async-start | bytes 196608 | tf_op jit(solution)/shard_map/all_to_all | solution.py:19
  213.4 316.2 %all-reduce.4.cloned.1.call-start = ((), (), s32[]{:S(2)}) async-start(), calls=%async_computation.4 | async-start | bytes 10485760
  233.5 6.2 %copy-start.4 = (f32[256]{0:T(256)S(1)}, f32[256]{0:T(256)}, u32[]{:S(2)}) copy-start(f32[256]{0:T(256)} %copy-done.3) | copy-start | bytes 3076
  233.5 6.2 %copy-start.6 = (f32[256]{0:T(256)S(1)}, f32[256]{0:T(256)}, u32[]{:S(2)}) copy-start(f32[256]{0:T(256)} %copy-done.5) | copy-start | bytes 3076
Sparse Core Ops, SparseCore 0:
  263.3 266.2 all-reduce.3
where the time goes:
time: 541 us; the launch traced here: 539 us
  waiting for transfers between devices  231 us (43%)
  blocking collectives  206 us (38%)
  local copies, waits for them, and re-layouts  40 us (7%)
  starting transfers between devices  19.3 us (4%)
  between operations  16.7 us (3%)
  matrix products  15.3 us (3%)
  other arithmetic  10.8 us (2%)
    unnamed x2, waiting for transfers between devices  226 us
    all_gather x1, blocking collectives, sent_together(): out, at, done = (lax.all_gather(both, axis, axis=dim, tiled=True), 0, [])  158 us
    psum x5, blocking collectives, one_axis_at_a_time(): shard = lax.psum(shard, axis)  39.2 us
    all_to_all x2, starting transfers between devices, from_everyone(): return lax.all_to_all(copies, axis, split_axis=0, concat_axis=0, tiled=True)  19.2 us
  transfers between devices with their start and end apart: 3, of which 2 were waited for; matrix products, arithmetic and copies ran while one was open for 2% of the time, Pallas kernels for 0%

commit v1 on v0

v1 whole, which is shorter than its diff:
```python
import math

import jax
import jax.numpy as jnp
from jax import lax
from jax.experimental import pallas as pl
from jax.experimental.pallas import tpu as pltpu
from jax.sharding import PartitionSpec as P

MESH = pl.DeviceIdType.MESH
BF16 = jnp.bfloat16
F32 = jnp.float32

NX, NY, NZ = 4, 4, 8
D, FF, LEN = 768, 1536, 128
GROUP = 128
NORM_EPS = 1e-06
HARD_BOOST = 1.5
CHUNKS = 6
CH = FF // CHUNKS
YB = FF // NY
XB = YB // 2 // NX
HALF = D // 2
OWN = XB // NZ


def nt(left, right):
    return lax.dot_general(left, right, (((1,), (1,)), ((), ())), preferred_element_type=F32)


def nn(left, right):
    return lax.dot_general(left, right, (((1,), (0,)), ((), ())), preferred_element_type=F32)


def cdf(v):
    return 0.5 * (1.0 + lax.erf(v * (1.0 / math.sqrt(2.0))))


def iota(shape, dim):
    return lax.broadcasted_iota(jnp.int32, shape, dim)


def kernel(
    pos_ref, hard_ref, q_hbm, p_hbm, wup_hbm, wdn_hbm,
    out_ref, loss_ref,
    x_v, wup_v, wdn_v, wupp_v, wdnp_v, hid_v, normed_v, scale_v, slope_v, gr_v,
    gb, gf, qall, pall,
    ts, cr, tf, ra, rb, oa, ob, rcv_a, rcv_b, sec_a, sec_b, s2a, s2b, r2a, r2b, zs, zr, lsend, lrecv,
    sem_in, z_s, z_r, g_s, g_r, c_s, c_r, l_s, l_r, core_s, core_r, a_s, a_r, b_s, b_r, x2_s, x2_r, y2_s, y2_r, zz_s, zz_r,
):
    dp = lax.axis_index("dp")
    xh = lax.axis_index("rep")
    core = lax.rem(dp, 2)
    z = lax.rem(lax.div(dp, 2), NZ)
    xl = lax.rem(lax.div(dp, 2 * NZ), 2)
    y = lax.div(dp, 4 * NZ)
    x = xh * 2 + xl

    def device(y_, x_, z_, core_):
        return (((y_ * 2 + lax.rem(x_, 2)) * NZ + z_) * 2 + core_, lax.div(x_, 2))

    def ymod(k):
        return lax.rem(y + k, NY)

    def xmod(k):
        return lax.rem(x + k, NX)

    def zmod(k):
        return lax.rem(z + k, NZ)

    partner = device(y, x, z, 1 - core)

    def plane(dy, dxl):
        xl_ = lax.rem(xl + dxl, 2)
        return ymod(dy), xl_, device(ymod(dy), xh * 2 + xl_, z, core)

    loads = []

    def load(src, dst):
        copy = pltpu.make_async_copy(src, dst, sem_in.at[len(loads)])
        copy.start()
        loads.append(copy)
        return copy

    x_loads = [load(q_hbm, x_v.at[0:LEN]), load(p_hbm, x_v.at[LEN : 2 * LEN])]
    up_loads = [load(wup_hbm.at[c * CH : (c + 1) * CH], wup_v.at[c * CH : (c + 1) * CH]) for c in range(CHUNKS)]
    dn_loads = [load(wdn_hbm.at[c * CH : (c + 1) * CH], wdn_v.at[c * CH : (c + 1) * CH]) for c in range(CHUNKS)]

    barrier = pltpu.get_barrier_semaphore()
    peers = [partner]
    peers += [device(y, x, zmod(k), core) for k in range(1, NZ)]
    peers += [plane(dy, dxl)[2] for dy in range(NY) for dxl in range(2) if dy or dxl]
    peers += [device(y, xmod(k), z, core) for k in range(1, NX)]
    for peer in peers:
        pl.semaphore_signal(barrier, inc=1, device_id=peer, device_id_type=MESH)

    for copy in x_loads:
        copy.wait()
    tokens = x_v[...]
    for c in range(CHUNKS):
        up_loads[c].wait()
        pre = nt(tokens, wup_v[c * CH : (c + 1) * CH, :])
        hid_v[:, c * CH : (c + 1) * CH] = (pre * cdf(pre)).astype(BF16)
    for copy in dn_loads:
        copy.wait()
    summed = tokens.astype(F32) + nn(hid_v[...], wdn_v[...])
    centred = summed - jnp.mean(summed, -1, keepdims=True)
    inv_scale = lax.rsqrt(jnp.mean(centred * centred, -1, keepdims=True) + NORM_EPS)
    normed = centred * inv_scale
    normed_v[...] = normed
    scale_v[...] = jnp.broadcast_to(inv_scale, (2 * LEN, 128))
    embed_q = jnp.sum(normed[:LEN], 0, keepdims=True) * (1.0 / LEN)
    embed_p = jnp.sum(normed[LEN:], 0, keepdims=True) * (1.0 / LEN)

    row = iota((16, 128), 0)
    lane = iota((16, 128), 1)
    tile = jnp.zeros((16, 128), F32)
    for k in range(6):
        tile = jnp.where(row == k, embed_q[:, k * 128 : (k + 1) * 128], tile)
        tile = jnp.where(row == 6 + k, embed_p[:, k * 128 : (k + 1) * 128], tile)
    named = jnp.where(lane == 0, pos_ref[0, 0], jnp.where(lane == 1, hard_ref[0, 0], hard_ref[0, 1]))
    tile = jnp.where(row == 12, named.astype(F32), tile)
    gb[y, xl, core, z] = tile.astype(BF16)

    pl.semaphore_wait(barrier, len(peers))

    def remote(src, dst, send, recv, to):
        return pltpu.make_async_remote_copy(
            src_ref=src, dst_ref=dst, send_sem=send, recv_sem=recv, device_id=to, device_id_type=MESH
        )

    sends = []
    own_tile = gb.at[y, xl, core, z]
    for k in range(1, NZ):
        copy = remote(own_tile, own_tile, z_s.at[k], z_r.at[k], device(y, x, zmod(k), core))
        copy.start()
        sends.append(copy)

    out_row = iota((YB, YB), 0)
    in_row = iota((YB, YB), 1)
    unit = lax.shift_right_logical(out_row * 10923, 16)
    inner = out_row - unit * 6
    slot_z = jnp.bitwise_and(unit, 7)
    slot_x = jnp.bitwise_and(lax.shift_right_logical(unit, 3), 3)
    slot_c = lax.shift_right_logical(unit, 5)
    to_z = jnp.bitwise_and(slot_z + z, 7)
    to_x = jnp.bitwise_and(slot_x + x, 3)
    to_c = jnp.where(slot_c == 0, 1 - core, core)
    to_xh = lax.shift_right_logical(to_x, 1)
    to_xl = jnp.bitwise_and(to_x, 1)
    source = (((to_xl * NZ + to_z) * 2 + to_c) * 2 + to_xh) * 6 + inner
    reorder = (source == in_row).astype(F32).astype(BF16)
    for sy in range(NY):
        rows = pl.ds(pl.multiple_of(ymod(sy) * YB, YB), YB)
        wdnp_v[sy] = nn(reorder, wdn_v[rows, :]).astype(BF16)

    for k in range(1, NZ):
        landed = gb.at[y, xl, core, zmod(NZ - k)]
        remote(landed, landed, z_s.at[k], z_r.at[k], device(y, x, zmod(k), core)).wait_recv()
    own_line = gb.at[y, xl, core]
    copy = remote(own_line, own_line, c_s.at[0], c_r.at[0], partner)
    copy.start()
    sends.append(copy)
    offsets = [(0, 1), (1, 0), (3, 0), (1, 1), (3, 1), (2, 0), (2, 1)]
    for dy, dxl in offsets:
        copy = remote(own_line, own_line, g_s.at[dy * 2 + dxl], g_r.at[dy * 2 + dxl], plane(dy, dxl)[2])
        copy.start()
        sends.append(copy)

    for sy in range(NY):
        rows = pl.ds(pl.multiple_of(ymod(sy) * YB, YB), YB)
        wupp_v[sy] = nn(reorder, wup_v[rows, :]).astype(BF16)
        pre = nt(wupp_v[sy], tokens)
        slope_v[sy] = cdf(pre) + pre * jnp.exp(-0.5 * pre * pre) * (1.0 / math.sqrt(2.0 * math.pi))

    for dy, dxl in offsets:
        y_, xl_, _ = plane(NY - dy, dxl)
        landed = gb.at[y_, xl_, core]
        remote(landed, landed, g_s.at[dy * 2 + dxl], g_r.at[dy * 2 + dxl], partner).wait_recv()
        copy = remote(landed, landed, c_s.at[dy * 2 + dxl], c_r.at[dy * 2 + dxl], partner)
        copy.start()
        sends.append(copy)
    for dy, dxl in [(0, 0)] + offsets:
        y_, xl_, _ = plane(NY - dy, dxl)
        landed = gb.at[y_, xl_, 1 - core]
        remote(landed, landed, c_s.at[dy * 2 + dxl], c_r.at[dy * 2 + dxl], partner).wait_recv()

    gf[...] = gb[...].reshape(GROUP * 16, 128).astype(F32)
    for k in range(6):
        qall[:, k * 128 : (k + 1) * 128] = gf[pl.ds(k, GROUP, stride=16), :].astype(BF16)
        pall[:, k * 128 : (k + 1) * 128] = gf[pl.ds(6 + k, GROUP, stride=16), :].astype(BF16)
    names = gf[pl.ds(12, GROUP, stride=16), :]
    scores = nt(qall[...], pall[...])
    place = iota((GROUP, GROUP), 1)
    group_index = (
        lax.shift_right_logical(place, 4) * 16
        + jnp.bitwise_and(place, 7) * 2
        + jnp.bitwise_and(lax.shift_right_logical(place, 3), 1)
    ).astype(F32)
    target = names[:, 0:1] == group_index
    hard = (names[:, 1:2] == group_index) | (names[:, 2:3] == group_index)
    logits = scores + jnp.where(hard, HARD_BOOST, 0.0)
    row_max = jnp.max(logits, -1, keepdims=True)
    log_total = row_max + jnp.log(jnp.sum(jnp.exp(logits - row_max), -1, keepdims=True))
    picked = jnp.sum(jnp.where(target, logits, 0.0), -1, keepdims=True)
    loss_sum = jnp.sum(log_total - picked, 0, keepdims=True)
    lsend[...] = jnp.broadcast_to(loss_sum, (8, 128))
    weights = (jnp.exp(logits - log_total) - jnp.where(target, 1.0, 0.0)).astype(BF16)
    mine = ((y * 2 + xl) * 2 + core) * NZ + z
    pick = (iota((16, GROUP), 1) == mine).astype(F32).astype(BF16)
    own_row = nn(pick, weights).astype(BF16)
    own_col = nt(pick, weights).astype(BF16)
    grad_q = nn(own_row, pall[...])[0:1] * (1.0 / LEN)
    grad_p = nn(own_col, qall[...])[0:1] * (1.0 / LEN)

    other = device(y, xmod(2), z, core)
    loss_copy = remote(lsend, lrecv, l_s.at[0], l_r.at[0], other)
    loss_copy.start()
    sends.append(loss_copy)

    for part, grad in ((0, grad_q), (1, grad_p)):
        rows = slice(part * LEN, (part + 1) * LEN)
        normed = normed_v[rows, :]
        along = jnp.mean(normed * grad, -1, keepdims=True)
        resid = grad - jnp.mean(grad, -1, keepdims=True) - normed * along
        gr_v[rows, :] = (scale_v[rows, 0:1] * resid).astype(BF16)
    resid = gr_v[...]
    order = (2, 1, 3, 0)
    core_copies = {}
    for sy in order:
        grad_pre = (nt(wdnp_v[sy], resid) * slope_v[sy]).astype(BF16)
        terms = nn(grad_pre, tokens)
        ts[sy] = terms[: YB // 2].reshape(NX, XB, D).astype(BF16)
        tf[sy] = terms[YB // 2 :].reshape(NX, XB, D)
        copy = remote(ts.at[sy], cr.at[sy], core_s.at[sy], core_r.at[sy], partner)
        copy.start()
        core_copies[sy] = copy
        sends.append(copy)

    y_up, y_dn = device(ymod(1), x, z, core), device(ymod(3), x, z, core)
    x_up, x_dn = device(y, xmod(1), z, core), device(y, xmod(3), z, core)
    colours = {"a": (ra, rcv_a, a_s, a_r, y_up, y_dn), "b": (rb, rcv_b, b_s, b_r, x_up, x_dn)}
    ring = {}

    def ring_send(colour, index, src):
        _, rcv, send, recv, up, down = colours[colour]
        to = up if index in (0, 1, 4) else down
        copy = remote(src, rcv.at[index], send.at[index], recv.at[index], to)
        copy.start()
        sends.append(copy)
        ring[colour, index] = copy

    for sy in order:
        core_copies[sy].wait_recv()
        got = tf[sy] + cr[sy].astype(F32)
        if sy == 0:
            oa[...] = got[:, :, :HALF]
        else:
            ra[sy] = got[:, :, :HALF].astype(BF16)
        ob[sy] = got[0, :, HALF:]
        for sx in range(1, NX):
            rb[sx, sy] = got[sx, :, HALF:].astype(BF16)
        if sy == 2:
            ring_send("a", 0, ra.at[2, 0:2])
            ring_send("a", 2, ra.at[2, 2:4])
        elif sy == 1:
            ring_send("a", 1, ra.at[1, 2:4])
        elif sy == 3:
            ring_send("a", 3, ra.at[3, 0:2])
            ring_send("b", 2, rb.at[2, 2:4])
            ring_send("b", 1, rb.at[1, 2:4])
        else:
            ring_send("b", 0, rb.at[2, 0:2])
            ring_send("b", 3, rb.at[3, 0:2])

    for colour, mid, sec in (("a", ra, sec_a), ("b", rb, sec_b)):
        rcv = colours[colour][1]
        ring[colour, 0].wait_recv()
        sec[0] = (mid[1, 0:2].astype(F32) + rcv[0].astype(F32)).astype(BF16)
        ring_send(colour, 4, sec.at[0])
        ring[colour, 2].wait_recv()
        sec[1] = (mid[3, 2:4].astype(F32) + rcv[2].astype(F32)).astype(BF16)
        ring_send(colour, 5, sec.at[1])

    second = {}
    for colour, own, s2, r2, send, recv in (("a", oa, s2a, r2a, x2_s, x2_r), ("b", ob, s2b, r2b, y2_s, y2_r)):
        rcv = colours[colour][1]
        ring[colour, 1].wait_recv()
        ring[colour, 3].wait_recv()
        ring[colour, 4].wait_recv()
        ring[colour, 5].wait_recv()
        own[0:2] = own[0:2] + rcv[3].astype(F32) + rcv[4].astype(F32)
        own[2:4] = own[2:4] + rcv[1].astype(F32) + rcv[5].astype(F32)
        for k in (2, 1, 3):
            s2[k] = own[k].astype(BF16)
            to = device(y, xmod(k), z, core) if colour == "a" else device(ymod(k), x, z, core)
            copy = remote(s2.at[k], r2.at[k], send.at[k], recv.at[k], to)
            copy.start()
            sends.append(copy)
            second[colour, k] = copy

    sums = []
    for colour, own, r2 in (("a", oa, r2a), ("b", ob, r2b)):
        total = own[0]
        for k in (1, 3, 2):
            second[colour, k].wait_recv()
            total = total + r2[k].astype(F32)
        sums.append(total)
    total = jnp.concatenate(sums, -1)

    spread_row = iota((NZ * 8, XB), 0)
    spread_of = lax.shift_right_logical(spread_row, 3) * OWN + jnp.bitwise_and(spread_row, 7)
    spread = (spread_of == iota((NZ * 8, XB), 1)) & (jnp.bitwise_and(spread_row, 7) < OWN)
    zs[...] = nn(spread.astype(F32).astype(BF16), total.astype(BF16)).reshape(NZ, 8, D).astype(BF16)
    last = []
    for k in (4, 3, 5, 2, 6, 1, 7):
        copy = remote(zs.at[k], zr.at[k], zz_s.at[k], zz_r.at[k], device(y, x, zmod(k), core))
        copy.start()
        sends.append(copy)
        last.append((k, copy))
    loss_copy.wait_recv()
    loss_ref[...] = (lsend[0:1, 0:1] + lrecv[0:1, 0:1]) * (1.0 / (2 * GROUP))
    final = total[0:OWN]
    for k, copy in reversed(last):
        copy.wait_recv()
        final = final + zr[k].astype(F32)[0:OWN]
    out_ref[...] = final
    for copy in sends:
        copy.wait_send()


def shards(q_hidden, p_hidden, w_up, w_down, pos_index, hard_index):
    vm = pltpu.VMEM
    dma = pltpu.SemaphoreType.DMA
    scratch = [
        vm((2 * LEN, D), BF16), vm((FF, D), BF16), vm((FF, D), BF16),
        vm((NY, YB, D), BF16), vm((NY, YB, D), BF16), vm((2 * LEN, FF), BF16),
        vm((2 * LEN, D), F32), vm((2 * LEN, 128), F32), vm((NY, YB, 2 * LEN), F32), vm((2 * LEN, D), BF16),
        vm((NY, 2, 2, NZ, 16, 128), BF16), vm((GROUP * 16, 128), F32), vm((GROUP, D), BF16), vm((GROUP, D), BF16),
        vm((NY, NX, XB, D), BF16), vm((NY, NX, XB, D), BF16), vm((NY, NX, XB, D), F32),
        vm((NY, NX, XB, HALF), BF16), vm((NX, NY, XB, HALF), BF16),
        vm((NX, XB, HALF), F32), vm((NY, XB, HALF), F32),
        vm((6, 2, XB, HALF), BF16), vm((6, 2, XB, HALF), BF16),
        vm((2, 2, XB, HALF), BF16), vm((2, 2, XB, HALF), BF16),
        vm((4, XB, HALF), BF16), vm((4, XB, HALF), BF16), vm((4, XB, HALF), BF16), vm((4, XB, HALF), BF16),
        vm((NZ, 8, D), BF16), vm((NZ, 8, D), BF16), vm((8, 128), F32), vm((8, 128), F32),
        dma((2 + 2 * CHUNKS,)), dma((8,)), dma((8,)), dma((8,)), dma((8,)), dma((8,)), dma((8,)), dma((1,)), dma((1,)),
        dma((4,)), dma((4,)), dma((6,)), dma((6,)), dma((6,)), dma((6,)),
        dma((4,)), dma((4,)), dma((4,)), dma((4,)), dma((8,)), dma((8,)),
    ]
    hbm = pl.BlockSpec(memory_space=pl.ANY)
    smem = pl.BlockSpec(memory_space=pltpu.SMEM)
    out, loss = pl.pallas_call(
        kernel,
        out_shape=(jax.ShapeDtypeStruct((OWN, D), F32), jax.ShapeDtypeStruct((1, 1), F32)),
        in_specs=[smem, smem, hbm, hbm, hbm, hbm],
        out_specs=(pl.BlockSpec(memory_space=pltpu.VMEM), pl.BlockSpec(memory_space=pltpu.VMEM)),
        scratch_shapes=scratch,
        compiler_params=pltpu.CompilerParams(
            collective_id=0, has_side_effects=True, vmem_limit_bytes=56 * 1024 * 1024
        ),
    )(pos_index, hard_index[0], q_hidden[0, 0], p_hidden[0, 0], w_up, w_down)
    return out, loss[0, 0]


def solution(mesh):
    return jax.shard_map(
        shards,
        mesh=mesh,
        in_specs=(
            P("rep", "dp", None, None),
            P("rep", "dp", None, None),
            P(),
            P(),
            P("rep", "dp"),
            P("rep", "dp", None),
        ),
        out_specs=(P(("dp", "rep"), None), P()),
        check_vma=False,
    )
```

time: 541 us -> 50.1 us (0.09)
  the two profiles are of different devices: /device:TPU:1 before, /device:TPU:8 now
where the time goes in v1:
time: 50.1 us; the launch traced here: 49.9 us
  Pallas kernels  45.5 us (91%)
  between operations  3.05 us (6%)
  local copies, waits for them, and re-layouts  1.35 us (3%)
    pallas_call x1, Pallas kernels, shards(): pl.pallas_call(kernel, out_shape=(jax.ShapeDtypeStruct((OWN, D), F32), ja...  45.5 us
    unnamed x1, local copies, waits for them, and re-layouts  1.35 us

profile of v1, /device:TPU:8, one launch (start us, length us, event | category | flops | bytes accessed | tf_op | source)
XLA Modules:
  0.0 49.9 jit_solution(14148738501958955939)
XLA Ops:
  1.3 45.5 %shard_map.77 = (f32[6,768]{1,0:T(8,128)}, f32[1,1]{1,0:T(1,128)}) custom-call(s32[1,1]{1,0:T(1,128)S(6)} %copy.10.pos_ref, s32[1,2]{1,0:T(1,128)} %bitcast.6, bf16[128,768]{1,0:T(8,128)(2,1)} %bitcast.4, bf16[128,768]{1,0:T(8,128)(2,1)} %bitcast.5, bf16[1536,768]{1,0:T(8,128)(2,1)} %wup_hbm.1, bf16[1536,768]{1,0:T(8,128)(2,1)} %wdn_hbm.1), custom_call_target="tpu_custom_call" | custom-call | tf_op jit(solution)/shard_map/pallas_call | solution.py:353
  46.8 1.3 %copy.11 = f32[6,768]{1,0:T(8,128)} copy(f32[6,768]{1,0:T(8,128)} %get-tuple-element.8) | data formatting | bytes 36864

commit v2 on v1

--- a/solution.py
+++ b/solution.py
@@ -19,9 +19,12 @@
 CHUNKS = 6
 CH = FF // CHUNKS
 YB = FF // NY
-XB = YB // 2 // NX
+CB = YB // 2
+XB = CB // NX
+ORDER = (2, 3, 1, 0)
 HALF = D // 2
 OWN = XB // NZ
+VMEM_LIMIT = 56 * 1024 * 1024
 
 
 def nt(left, right):
@@ -41,11 +44,11 @@
 
 
 def kernel(
-    pos_ref, hard_ref, q_hbm, p_hbm, wup_hbm, wdn_hbm,
+    pos_hbm, hard_hbm, q_hbm, p_hbm, wup_hbm, wdn_hbm,
     out_ref, loss_ref,
-    x_v, wup_v, wdn_v, wupp_v, wdnp_v, hid_v, normed_v, scale_v, slope_v, gr_v,
+    pos_ref, hard_ref, x_v, wup_v, wdn_v, wupp_v, wdnp_v, hid_v, normed_v, scale_v, slope_v, gr_v,
     gb, gf, qall, pall,
-    ts, cr, tf, ra, rb, oa, ob, rcv_a, rcv_b, sec_a, sec_b, s2a, s2b, r2a, r2b, zs, zr, lsend, lrecv,
+    ra, rb, oa, ob, rcv_a, rcv_b, sec_a, sec_b, s2a, s2b, r2a, r2b, zs, zr, lsend, lrecv,
     sem_in, z_s, z_r, g_s, g_r, c_s, c_r, l_s, l_r, core_s, core_r, a_s, a_r, b_s, b_r, x2_s, x2_r, y2_s, y2_r, zz_s, zz_r,
 ):
     dp = lax.axis_index("dp")
@@ -84,6 +87,7 @@
 
     x_loads = [load(q_hbm, x_v.at[0:LEN]), load(p_hbm, x_v.at[LEN : 2 * LEN])]
     up_loads = [load(wup_hbm.at[c * CH : (c + 1) * CH], wup_v.at[c * CH : (c + 1) * CH]) for c in range(CHUNKS)]
+    index_loads = [load(pos_hbm, pos_ref), load(hard_hbm, hard_ref)]
     dn_loads = [load(wdn_hbm.at[c * CH : (c + 1) * CH], wdn_v.at[c * CH : (c + 1) * CH]) for c in range(CHUNKS)]
 
     barrier = pltpu.get_barrier_semaphore()
@@ -96,7 +100,7 @@
 
     for copy in x_loads:
         copy.wait()
-    tokens = x_v[...]
+    tokens = x_v[: 2 * LEN, :]
     for c in range(CHUNKS):
         up_loads[c].wait()
         pre = nt(tokens, wup_v[c * CH : (c + 1) * CH, :])
@@ -107,11 +111,13 @@
     centred = summed - jnp.mean(summed, -1, keepdims=True)
     inv_scale = lax.rsqrt(jnp.mean(centred * centred, -1, keepdims=True) + NORM_EPS)
     normed = centred * inv_scale
-    normed_v[...] = normed
-    scale_v[...] = jnp.broadcast_to(inv_scale, (2 * LEN, 128))
+    normed_v[: 2 * LEN, :] = normed.astype(BF16)
+    scale_v[: 2 * LEN, :] = jnp.broadcast_to(inv_scale, (2 * LEN, 128))
     embed_q = jnp.sum(normed[:LEN], 0, keepdims=True) * (1.0 / LEN)
     embed_p = jnp.sum(normed[LEN:], 0, keepdims=True) * (1.0 / LEN)
 
+    for copy in index_loads:
+        copy.wait()
     row = iota((16, 128), 0)
     lane = iota((16, 128), 1)
     tile = jnp.zeros((16, 128), F32)
@@ -136,23 +142,30 @@
         copy.start()
         sends.append(copy)
 
-    out_row = iota((YB, YB), 0)
-    in_row = iota((YB, YB), 1)
+    shared = []
+    for k, buf in enumerate((x_v, normed_v, scale_v)):
+        copy = remote(
+            buf.at[: 2 * LEN], buf.at[2 * LEN :], core_s.at[k], core_r.at[k], partner
+        )
+        copy.start()
+        shared.append(copy)
+        sends.append(copy)
+
+    out_row = iota((CB, YB), 0)
+    in_row = iota((CB, YB), 1)
     unit = lax.shift_right_logical(out_row * 10923, 16)
     inner = out_row - unit * 6
     slot_z = jnp.bitwise_and(unit, 7)
-    slot_x = jnp.bitwise_and(lax.shift_right_logical(unit, 3), 3)
-    slot_c = lax.shift_right_logical(unit, 5)
+    slot_x = lax.shift_right_logical(unit, 3)
     to_z = jnp.bitwise_and(slot_z + z, 7)
     to_x = jnp.bitwise_and(slot_x + x, 3)
-    to_c = jnp.where(slot_c == 0, 1 - core, core)
     to_xh = lax.shift_right_logical(to_x, 1)
     to_xl = jnp.bitwise_and(to_x, 1)
-    source = (((to_xl * NZ + to_z) * 2 + to_c) * 2 + to_xh) * 6 + inner
+    source = (((to_xl * NZ + to_z) * 2 + core) * 2 + to_xh) * 6 + inner
     reorder = (source == in_row).astype(F32).astype(BF16)
-    for sy in range(NY):
+    for i, sy in enumerate(ORDER):
         rows = pl.ds(pl.multiple_of(ymod(sy) * YB, YB), YB)
-        wdnp_v[sy] = nn(reorder, wdn_v[rows, :]).astype(BF16)
+        wdnp_v[i * CB : (i + 1) * CB, :] = nn(reorder, wdn_v[rows, :]).astype(BF16)
 
     for k in range(1, NZ):
         landed = gb.at[y, xl, core, zmod(NZ - k)]
@@ -167,11 +180,16 @@
         copy.start()
         sends.append(copy)
 
-    for sy in range(NY):
+    for i, sy in enumerate(ORDER):
         rows = pl.ds(pl.multiple_of(ymod(sy) * YB, YB), YB)
-        wupp_v[sy] = nn(reorder, wup_v[rows, :]).astype(BF16)
-        pre = nt(wupp_v[sy], tokens)
-        slope_v[sy] = cdf(pre) + pre * jnp.exp(-0.5 * pre * pre) * (1.0 / math.sqrt(2.0 * math.pi))
+        wupp_v[i * CB : (i + 1) * CB, :] = nn(reorder, wup_v[rows, :]).astype(BF16)
+    for copy in shared:
+        copy.wait_recv()
+    both = x_v[...]
+    for i in range(2):
+        block = slice(i * YB, (i + 1) * YB)
+        pre = nt(wupp_v[block, :], both)
+        slope_v[block, :] = cdf(pre) + pre * jnp.exp(-0.5 * pre * pre) * (1.0 / math.sqrt(2.0 * math.pi))
 
     for dy, dxl in offsets:
         y_, xl_, _ = plane(NY - dy, dxl)
@@ -206,36 +224,26 @@
     loss_sum = jnp.sum(log_total - picked, 0, keepdims=True)
     lsend[...] = jnp.broadcast_to(loss_sum, (8, 128))
     weights = (jnp.exp(logits - log_total) - jnp.where(target, 1.0, 0.0)).astype(BF16)
-    mine = ((y * 2 + xl) * 2 + core) * NZ + z
-    pick = (iota((16, GROUP), 1) == mine).astype(F32).astype(BF16)
+    mine = (y * 2 + xl) * 2 * NZ + z
+    pick_core = jnp.where(iota((16, GROUP), 0) < 8, core, 1 - core)
+    pick = (iota((16, GROUP), 1) == mine + pick_core * NZ).astype(F32).astype(BF16)
     own_row = nn(pick, weights).astype(BF16)
     own_col = nt(pick, weights).astype(BF16)
-    grad_q = nn(own_row, pall[...])[0:1] * (1.0 / LEN)
-    grad_p = nn(own_col, qall[...])[0:1] * (1.0 / LEN)
+    grad_q = nn(own_row, pall[...]) * (1.0 / LEN)
+    grad_p = nn(own_col, qall[...]) * (1.0 / LEN)
 
     other = device(y, xmod(2), z, core)
     loss_copy = remote(lsend, lrecv, l_s.at[0], l_r.at[0], other)
     loss_copy.start()
     sends.append(loss_copy)
 
-    for part, grad in ((0, grad_q), (1, grad_p)):
+    for part, grad in enumerate((grad_q[0:1], grad_p[0:1], grad_q[8:9], grad_p[8:9])):
         rows = slice(part * LEN, (part + 1) * LEN)
-        normed = normed_v[rows, :]
-        along = jnp.mean(normed * grad, -1, keepdims=True)
-        resid = grad - jnp.mean(grad, -1, keepdims=True) - normed * along
-        gr_v[rows, :] = (scale_v[rows, 0:1] * resid).astype(BF16)
+        normed = normed_v[rows, :].astype(F32)
+        offset = grad - jnp.mean(grad, -1, keepdims=True)
+        along = jnp.mean(normed * offset, -1, keepdims=True)
+        gr_v[rows, :] = (scale_v[rows, 0:1] * (offset - normed * along)).astype(BF16)
     resid = gr_v[...]
-    order = (2, 1, 3, 0)
-    core_copies = {}
-    for sy in order:
-        grad_pre = (nt(wdnp_v[sy], resid) * slope_v[sy]).astype(BF16)
-        terms = nn(grad_pre, tokens)
-        ts[sy] = terms[: YB // 2].reshape(NX, XB, D).astype(BF16)
-        tf[sy] = terms[YB // 2 :].reshape(NX, XB, D)
-        copy = remote(ts.at[sy], cr.at[sy], core_s.at[sy], core_r.at[sy], partner)
-        copy.start()
-        core_copies[sy] = copy
-        sends.append(copy)
 
     y_up, y_dn = device(ymod(1), x, z, core), device(ymod(3), x, z, core)
     x_up, x_dn = device(y, xmod(1), z, core), device(y, xmod(3), z, core)
@@ -250,23 +258,26 @@
         sends.append(copy)
         ring[colour, index] = copy
 
-    for sy in order:
-        core_copies[sy].wait_recv()
-        got = tf[sy] + cr[sy].astype(F32)
-        if sy == 0:
-            oa[...] = got[:, :, :HALF]
-        else:
-            ra[sy] = got[:, :, :HALF].astype(BF16)
-        ob[sy] = got[0, :, HALF:]
-        for sx in range(1, NX):
-            rb[sx, sy] = got[sx, :, HALF:].astype(BF16)
-        if sy == 2:
-            ring_send("a", 0, ra.at[2, 0:2])
-            ring_send("a", 2, ra.at[2, 2:4])
-        elif sy == 1:
-            ring_send("a", 1, ra.at[1, 2:4])
-        elif sy == 3:
-            ring_send("a", 3, ra.at[3, 0:2])
+    for i in range(2):
+        block = slice(i * YB, (i + 1) * YB)
+        grad_pre = (nt(wdnp_v[block, :], resid) * slope_v[block, :]).astype(BF16)
+        pair = nn(grad_pre, both).reshape(2, NX, XB, D)
+        for sy, terms in zip(ORDER[2 * i : 2 * i + 2], (pair[0], pair[1])):
+            if sy == 0:
+                oa[...] = terms[:, :, :HALF]
+            else:
+                ra[sy] = terms[:, :, :HALF].astype(BF16)
+            if sy == 2:
+                ring_send("a", 0, ra.at[2, 0:2])
+                ring_send("a", 2, ra.at[2, 2:4])
+            elif sy == 1:
+                ring_send("a", 1, ra.at[1, 2:4])
+            elif sy == 3:
+                ring_send("a", 3, ra.at[3, 0:2])
+            ob[sy] = terms[0, :, HALF:]
+            for sx in range(1, NX):
+                rb[sx, sy] = terms[sx, :, HALF:].astype(BF16)
+        if i == 0:
             ring_send("b", 2, rb.at[2, 2:4])
             ring_send("b", 1, rb.at[1, 2:4])
         else:
@@ -333,31 +344,30 @@
     vm = pltpu.VMEM
     dma = pltpu.SemaphoreType.DMA
     scratch = [
-        vm((2 * LEN, D), BF16), vm((FF, D), BF16), vm((FF, D), BF16),
-        vm((NY, YB, D), BF16), vm((NY, YB, D), BF16), vm((2 * LEN, FF), BF16),
-        vm((2 * LEN, D), F32), vm((2 * LEN, 128), F32), vm((NY, YB, 2 * LEN), F32), vm((2 * LEN, D), BF16),
+        pltpu.SMEM((1, 1), jnp.int32), pltpu.SMEM((1, 2), jnp.int32),
+        vm((4 * LEN, D), BF16), vm((FF, D), BF16), vm((FF, D), BF16),
+        vm((FF // 2, D), BF16), vm((FF // 2, D), BF16), vm((2 * LEN, FF), BF16),
+        vm((4 * LEN, D), BF16), vm((4 * LEN, 128), F32), vm((FF // 2, 4 * LEN), F32), vm((4 * LEN, D), BF16),
         vm((NY, 2, 2, NZ, 16, 128), BF16), vm((GROUP * 16, 128), F32), vm((GROUP, D), BF16), vm((GROUP, D), BF16),
-        vm((NY, NX, XB, D), BF16), vm((NY, NX, XB, D), BF16), vm((NY, NX, XB, D), F32),
         vm((NY, NX, XB, HALF), BF16), vm((NX, NY, XB, HALF), BF16),
         vm((NX, XB, HALF), F32), vm((NY, XB, HALF), F32),
         vm((6, 2, XB, HALF), BF16), vm((6, 2, XB, HALF), BF16),
         vm((2, 2, XB, HALF), BF16), vm((2, 2, XB, HALF), BF16),
         vm((4, XB, HALF), BF16), vm((4, XB, HALF), BF16), vm((4, XB, HALF), BF16), vm((4, XB, HALF), BF16),
         vm((NZ, 8, D), BF16), vm((NZ, 8, D), BF16), vm((8, 128), F32), vm((8, 128), F32),
-        dma((2 + 2 * CHUNKS,)), dma((8,)), dma((8,)), dma((8,)), dma((8,)), dma((8,)), dma((8,)), dma((1,)), dma((1,)),
+        dma((4 + 2 * CHUNKS,)), dma((8,)), dma((8,)), dma((8,)), dma((8,)), dma((8,)), dma((8,)), dma((1,)), dma((1,)),
         dma((4,)), dma((4,)), dma((6,)), dma((6,)), dma((6,)), dma((6,)),
         dma((4,)), dma((4,)), dma((4,)), dma((4,)), dma((8,)), dma((8,)),
     ]
-    hbm = pl.BlockSpec(memory_space=pl.ANY)
-    smem = pl.BlockSpec(memory_space=pltpu.SMEM)
+    hbm = pl.BlockSpec(memory_space=pltpu.HBM)
     out, loss = pl.pallas_call(
         kernel,
-        out_shape=(jax.ShapeDtypeStruct((OWN, D), F32), jax.ShapeDtypeStruct((1, 1), F32)),
-        in_specs=[smem, smem, hbm, hbm, hbm, hbm],
+        out_shape=(pltpu.VMEM((OWN, D), F32), pltpu.VMEM((1, 1), F32)),
+        in_specs=[hbm, hbm, hbm, hbm, hbm, hbm],
         out_specs=(pl.BlockSpec(memory_space=pltpu.VMEM), pl.BlockSpec(memory_space=pltpu.VMEM)),
         scratch_shapes=scratch,
         compiler_params=pltpu.CompilerParams(
-            collective_id=0, has_side_effects=True, vmem_limit_bytes=56 * 1024 * 1024
+            collective_id=0, has_side_effects=True, vmem_limit_bytes=VMEM_LIMIT
         ),
     )(pos_index, hard_index[0], q_hidden[0, 0], p_hidden[0, 0], w_up, w_down)
     return out, loss[0, 0]

time: 50.1 us -> 45.8 us (0.914)
  the two profiles are of different devices: /device:TPU:8 before, /device:TPU:1 now
where the time goes in v2:
time: 45.8 us; the launch traced here: 45.7 us
  Pallas kernels  42.7 us (93%)
  between operations  2.45 us (5%)
  local copies, waits for them, and re-layouts  0.61 us (1%)
    pallas_call x1, Pallas kernels, shards(): pl.pallas_call(kernel, out_shape=(pltpu.VMEM((OWN, D), F32), pltpu.VMEM((...  42.7 us

profile of v2, /device:TPU:1, one launch (start us, length us, event | category | flops | bytes accessed | tf_op | source)
XLA Modules:
  0.0 45.7 jit_solution(9144021614788867085)
XLA Ops:
  1.3 42.7 %shard_map.77 = (f32[6,768]{1,0:T(8,128)S(1)}, f32[1,1]{1,0:T(1,128)S(1)}) custom-call(s32[1,1]{1,0:T(1,128)S(6)} %copy.12.pos_hbm, s32[1,2]{1,0:T(1,128)} %bitcast.6, bf16[128,768]{1,0:T(8,128)(2,1)} %bitcast.4, bf16[128,768]{1,0:T(8,128)(2,1)} %bitcast.5, bf16[1536,768]{1,0:T(8,128)(2,1)} %wup_hbm.1, bf16[1536,768]{1,0:T(8,128)(2,1)} %wdn_hbm.1), custom_call_target="tpu_custom_call" | custom-call | tf_op jit(solution)/shard_map/pallas_call | solution.py:363
  44.0 0.6 %copy.10 = f32[6,768]{1,0:T(8,128)} copy(f32[6,768]{1,0:T(8,128)S(1)} %get-tuple-element.6) | data formatting | bytes 36864

commit v3 on v2

v3 whole, which is shorter than its diff:
```python
import math

import jax
import jax.numpy as jnp
from jax import lax
from jax.experimental import pallas as pl
from jax.experimental.pallas import tpu as pltpu
from jax.sharding import PartitionSpec as P

MESH = pl.DeviceIdType.MESH
BF16 = jnp.bfloat16
F32 = jnp.float32

NX, NY, NZ = 4, 4, 8
D, FF, LEN = 768, 1536, 128
GROUP = 128
NORM_EPS = 1e-06
HARD_BOOST = 1.5
CHUNKS = 3
CH = FF // CHUNKS
YB = FF // NY
CB = YB // 2
XB = CB // NX
ORDER = (2, 1, 3, 0)
WIDE = D + 128
HALF = D // 2
OWN = XB // NZ
VMEM_LIMIT = 56 * 1024 * 1024


def nt(left, right):
    return lax.dot_general(left, right, (((1,), (1,)), ((), ())), preferred_element_type=F32)


def nn(left, right):
    return lax.dot_general(left, right, (((1,), (0,)), ((), ())), preferred_element_type=F32)


def cdf(v):
    return 0.5 * (1.0 + lax.erf(v * (1.0 / math.sqrt(2.0))))


def iota(shape, dim):
    return lax.broadcasted_iota(jnp.int32, shape, dim)


def kernel(
    pos_hbm, hard_hbm, q_hbm, p_hbm, wup_hbm, wdn_hbm,
    out_ref, loss_ref,
    pos_ref, hard_ref, x_v, wup_v, wdn_v, wupp_v, wdnp_v, normed_v, scale_v, slope_v, along_v,
    tiles, spread_v, gb, gp_v,
    ra, rb, oa, ob, rcv_a, rcv_b, sec_a, sec_b, s2a, s2b, r2a, r2b, zs, zr, lsend, lrecv,
    sem_in, z_s, z_r, g_s, g_r, c_s, c_r, l_s, l_r, core_s, core_r, a_s, a_r, b_s, b_r, x2_s, x2_r, y2_s, y2_r, zz_s, zz_r,
):
    dp = lax.axis_index("dp")
    xh = lax.axis_index("rep")
    core = lax.rem(dp, 2)
    z = lax.rem(lax.div(dp, 2), NZ)
    xl = lax.rem(lax.div(dp, 2 * NZ), 2)
    y = lax.div(dp, 4 * NZ)
    x = xh * 2 + xl

    def device(y_, x_, z_, core_):
        return (((y_ * 2 + lax.rem(x_, 2)) * NZ + z_) * 2 + core_, lax.div(x_, 2))

    def ymod(k):
        return lax.rem(y + k, NY)

    def xmod(k):
        return lax.rem(x + k, NX)

    def zmod(k):
        return lax.rem(z + k, NZ)

    partner = device(y, x, z, 1 - core)

    def plane(dy, dxl):
        xl_ = lax.rem(xl + dxl, 2)
        return ymod(dy), xl_, device(ymod(dy), xh * 2 + xl_, z, core)

    loads = []

    def load(src, dst):
        copy = pltpu.make_async_copy(src, dst, sem_in.at[len(loads)])
        copy.start()
        loads.append(copy)
        return copy

    x_loads = [load(q_hbm, x_v.at[0:LEN]), load(p_hbm, x_v.at[LEN : 2 * LEN])]
    up_loads = [load(wup_hbm.at[rows], wup_v.at[rows]) for rows in (slice(0, CH), slice(CH, FF))]
    dn_load = load(wdn_hbm, wdn_v)
    index_loads = [load(pos_hbm, pos_ref), load(hard_hbm, hard_ref)]

    barrier = pltpu.get_barrier_semaphore()
    peers = [partner]
    peers += [device(y, x, zmod(k), core) for k in range(1, NZ)]
    peers += [plane(dy, dxl)[2] for dy in range(NY) for dxl in range(2) if dy or dxl]
    peers += [device(y, xmod(k), z, core) for k in range(1, NX)]
    for peer in peers:
        pl.semaphore_signal(barrier, inc=1, device_id=peer, device_id_type=MESH)

    for copy in x_loads:
        copy.wait()
    tokens = x_v[: 2 * LEN, :]
    hidden, pre = [], None
    for c in range(CHUNKS):
        if c < 2:
            up_loads[c].wait()
        done, pre = pre, nt(tokens, wup_v[c * CH : (c + 1) * CH, :])
        if c:
            hidden.append((done * cdf(done)).astype(BF16))
    dn_load.wait()
    hidden.append((pre * cdf(pre)).astype(BF16))
    summed = tokens.astype(F32)
    for c in range(CHUNKS):
        summed = summed + nn(hidden[c], wdn_v[c * CH : (c + 1) * CH, :])
    centred = summed - jnp.mean(summed, -1, keepdims=True)
    inv_scale = lax.rsqrt(jnp.mean(centred * centred, -1, keepdims=True) + NORM_EPS)
    normed = centred * inv_scale
    normed_v[: 2 * LEN, :] = normed.astype(BF16)
    embed_q = jnp.sum(normed[:LEN], 0, keepdims=True) * (1.0 / LEN)
    embed_p = jnp.sum(normed[LEN:], 0, keepdims=True) * (1.0 / LEN)

    for copy in index_loads:
        copy.wait()
    row = iota((16, 128), 0)
    lane = iota((16, 128), 1)
    tile = jnp.zeros((16, 128), F32)
    for k in range(6):
        tile = jnp.where(row == k, embed_q[:, k * 128 : (k + 1) * 128], tile)
        tile = jnp.where(row == 6 + k, embed_p[:, k * 128 : (k + 1) * 128], tile)
    named = jnp.where(lane == 0, pos_ref[0, 0], jnp.where(lane == 1, hard_ref[0, 0], hard_ref[0, 1]))
    tile = jnp.where(row == 12, named.astype(F32), tile)
    tiles[z] = tile.astype(BF16)

    pl.semaphore_wait(barrier, len(peers))

    def remote(src, dst, send, recv, to):
        return pltpu.make_async_remote_copy(
            src_ref=src, dst_ref=dst, send_sem=send, recv_sem=recv, device_id=to, device_id_type=MESH
        )

    sends = []
    own_tile = tiles.at[z]
    for k in range(1, NZ):
        copy = remote(own_tile, own_tile, z_s.at[k], z_r.at[k], device(y, x, zmod(k), core))
        copy.start()
        sends.append(copy)

    scale_v[0] = jnp.transpose(jnp.broadcast_to(inv_scale, (2 * LEN, 128)))[0:8]
    shared = []
    for k, (own, theirs) in enumerate((
        (x_v.at[: 2 * LEN], x_v.at[2 * LEN :]),
        (normed_v.at[: 2 * LEN], normed_v.at[2 * LEN :]),
        (scale_v.at[0], scale_v.at[1]),
    )):
        copy = remote(own, theirs, core_s.at[k], core_r.at[k], partner)
        copy.start()
        shared.append(copy)
        sends.append(copy)

    out_row = iota((CB, YB), 0)
    in_row = iota((CB, YB), 1)
    unit = lax.shift_right_logical(out_row * 10923, 16)
    inner = out_row - unit * 6
    slot_z = jnp.bitwise_and(unit, 7)
    slot_x = lax.shift_right_logical(unit, 3)
    to_z = jnp.bitwise_and(slot_z + z, 7)
    to_x = jnp.bitwise_and(slot_x + x, 3)
    to_xh = lax.shift_right_logical(to_x, 1)
    to_xl = jnp.bitwise_and(to_x, 1)
    source = (((to_xl * NZ + to_z) * 2 + core) * 2 + to_xh) * 6 + inner
    reorder = (source == in_row).astype(F32).astype(BF16)
    for i, sy in enumerate(ORDER):
        rows = pl.ds(pl.multiple_of(ymod(sy) * YB, YB), YB)
        wdnp_v[i * CB : (i + 1) * CB, :] = nn(reorder, wdn_v[rows, :]).astype(BF16)
        wupp_v[i * CB : (i + 1) * CB, :] = nn(reorder, wup_v[rows, :]).astype(BF16)

    for k in range(1, NZ):
        landed = tiles.at[zmod(NZ - k)]
        remote(landed, landed, z_s.at[k], z_r.at[k], device(y, x, zmod(k), core)).wait_recv()
    spread_v[...] = tiles[...].reshape(NZ * 16, 128).astype(F32)
    own_line = gb.at[y, xl, core]
    for k in range(7):
        upper = spread_v[pl.ds(12 if k == 6 else k, NZ, stride=16), :]
        lower = spread_v[pl.ds(12 if k == 6 else 6 + k, NZ, stride=16), :]
        own_line[:, k * 128 : (k + 1) * 128] = jnp.concatenate([upper, lower], 0).astype(BF16)
    copy = remote(own_line, own_line, c_s.at[0], c_r.at[0], partner)
    copy.start()
    sends.append(copy)
    offsets = [(0, 1), (1, 0), (3, 0), (1, 1), (3, 1), (2, 0), (2, 1)]
    for dy, dxl in offsets:
        copy = remote(own_line, own_line, g_s.at[dy * 2 + dxl], g_r.at[dy * 2 + dxl], plane(dy, dxl)[2])
        copy.start()
        sends.append(copy)

    for copy in shared:
        copy.wait_recv()
    both = x_v[...]
    scale = jnp.concatenate([scale_v[0, 0:1, :], scale_v[1, 0:1, :]], 1)
    for i in range(2):
        block = slice(i * YB, (i + 1) * YB)
        pre = nt(wupp_v[block, :], both)
        slope = (cdf(pre) + pre * jnp.exp(-0.5 * pre * pre) * (1.0 / math.sqrt(2.0 * math.pi))) * scale
        slope_v[block, :] = slope
        along_v[block, :] = slope * nt(wdnp_v[block, :], normed_v[...])

    for dy, dxl in offsets:
        y_, xl_, _ = plane(NY - dy, dxl)
        landed = gb.at[y_, xl_, core]
        remote(landed, landed, g_s.at[dy * 2 + dxl], g_r.at[dy * 2 + dxl], partner).wait_recv()
        copy = remote(landed, landed, c_s.at[dy * 2 + dxl], c_r.at[dy * 2 + dxl], partner)
        copy.start()
        sends.append(copy)
    for dy, dxl in [(0, 0)] + offsets:
        y_, xl_, _ = plane(NY - dy, dxl)
        landed = gb.at[y_, xl_, 1 - core]
        remote(landed, landed, c_s.at[dy * 2 + dxl], c_r.at[dy * 2 + dxl], partner).wait_recv()

    everyone = gb[...].reshape(2 * GROUP, WIDE)
    sequences = everyone[:, :D]
    names = everyone[:, D:].astype(F32)
    scores = nt(sequences, sequences)
    place = iota((2 * GROUP, 2 * GROUP), 1)
    line = lax.shift_right_logical(place, 4)
    group_index = (
        lax.shift_right_logical(line, 1) * 16 + jnp.bitwise_and(place, 7) * 2 + jnp.bitwise_and(line, 1)
    ).astype(F32)
    is_passage = jnp.bitwise_and(place, 8) == 8
    target = (names[:, 0:1] == group_index) & is_passage
    hard = (names[:, 1:2] == group_index) | (names[:, 2:3] == group_index)
    logits = scores + jnp.where(hard, HARD_BOOST, 0.0)
    row_max = jnp.max(jnp.where(is_passage, logits, -jnp.inf), -1, keepdims=True)
    powers = jnp.where(is_passage, jnp.exp(logits - row_max), 0.0)
    power_sum = jnp.sum(powers, -1, keepdims=True)
    log_total = row_max + jnp.log(power_sum)
    picked = jnp.sum(jnp.where(target, logits, 0.0), -1, keepdims=True)
    row_is_query = jnp.bitwise_and(iota((2 * GROUP, 2 * GROUP), 0), 8) == 0
    loss_sum = jnp.sum(jnp.where(row_is_query[:, 0:1], log_total - picked, 0.0), 0, keepdims=True)
    lsend[...] = jnp.broadcast_to(loss_sum, (8, 128))
    softmax = jnp.where(is_passage, jnp.exp(logits - log_total), 0.0)
    weights = jnp.where(row_is_query, softmax - jnp.where(target, 1.0, 0.0), 0.0).astype(BF16)
    pick_row = iota((16, 2 * GROUP), 0)
    other_core = jnp.bitwise_and(lax.shift_right_logical(pick_row, 1), 1)
    pick_core = other_core + core - 2 * other_core * core
    pick_part = jnp.bitwise_and(pick_row, 1)
    mine = iota((16, 2 * GROUP), 1) == (((y * 2 + xl) * 2 + pick_core) * 2 + pick_part) * NZ + z
    own_row = nn((mine & (pick_part == 0)).astype(F32).astype(BF16), weights).astype(BF16)
    own_col = nt((mine & (pick_part == 1)).astype(F32).astype(BF16), weights).astype(BF16)
    grad = nn(own_row + own_col, sequences) * (1.0 / LEN)
    parts = (grad - jnp.mean(grad, -1, keepdims=True)).astype(BF16)

    other = device(y, xmod(2), z, core)
    loss_copy = remote(lsend, lrecv, l_s.at[0], l_r.at[0], other)
    loss_copy.start()
    sends.append(loss_copy)

    along_all = nt(parts, normed_v[...]) * (1.0 / D)
    across_all = nt(wdnp_v[...], parts)
    spans = [slice(k * LEN, (k + 1) * LEN) for k in range(4)]
    along = [along_all[k : k + 1, span] for k, span in enumerate(spans)]
    for i in range(4):
        block = slice(i * CB, (i + 1) * CB)
        for k, span in enumerate(spans):
            late = across_all[block, k : k + 1] * slope_v[block, span] - along[k] * along_v[block, span]
            gp_v[i, :, :, span] = late.astype(BF16).reshape(NX, XB, LEN)

    y_up, y_dn = device(ymod(1), x, z, core), device(ymod(3), x, z, core)
    x_up, x_dn = device(y, xmod(1), z, core), device(y, xmod(3), z, core)
    colours = {"a": (ra, rcv_a, a_s, a_r, y_up, y_dn), "b": (rb, rcv_b, b_s, b_r, x_up, x_dn)}
    ring = {}

    def ring_send(colour, index, src, rcv, up):
        _, _, send, recv, to_up, to_down = colours[colour]
        copy = remote(src, rcv, send.at[index], recv.at[index], to_up if up else to_down)
        copy.start()
        sends.append(copy)
        ring[colour, index] = copy

    def relay(colour, piece):
        mid, rcv = colours[colour][:2]
        ring_send(colour, piece, mid.at[2, piece], rcv.at[piece], piece < 2)

    def direct(colour, up):
        mid, rcv = colours[colour][:2]
        if up:
            ring_send(colour, 8, mid.at[1, 2:4], rcv.at[10:12], True)
        else:
            ring_send(colour, 9, mid.at[3, 0:2], rcv.at[8:10], False)

    def terms(rows, right):
        cols = slice(HALF, D) if right else slice(0, HALF)
        return nn(rows.reshape(-1, 4 * LEN), x_v[:, cols]).reshape(-1, 4, XB, HALF)

    ra[2] = terms(gp_v[0], False)[0].astype(BF16)
    for piece in (2, 1, 3, 0):
        relay("a", piece)
    far = terms(gp_v[:, 2], True)[0].astype(BF16)
    for i in range(4):
        rb[2, ORDER[i]] = far[i]
    for piece in (2, 1, 3, 0):
        relay("b", piece)
    near = terms(gp_v[1:3], False).astype(BF16)
    ra[1] = near[0]
    ra[3] = near[1]
    direct("a", True)
    direct("a", False)
    near = terms(jnp.concatenate([gp_v[:, 1], gp_v[:, 3]], 0), True).astype(BF16)
    for i in range(4):
        rb[1, ORDER[i]] = near[0, i]
        rb[3, ORDER[i]] = near[1, i]
    direct("b", True)
    direct("b", False)
    oa[...] = terms(gp_v[3], False)[0]
    home = terms(gp_v[:, 0], True)[0]
    for i in range(4):
        ob[ORDER[i]] = home[i]

    for colour, piece in (("a", 2), ("a", 1), ("b", 2), ("b", 1), ("a", 3), ("a", 0), ("b", 3), ("b", 0)):
        mid, rcv = colours[colour][:2]
        sec = sec_a if colour == "a" else sec_b
        ring[colour, piece].wait_recv()
        sec[piece] = (mid[1 if piece < 2 else 3, piece].astype(F32) + rcv[piece].astype(F32)).astype(BF16)
        ring_send(colour, 4 + piece, sec.at[piece], rcv.at[4 + piece], piece < 2)

    second = {}
    seconds = {"a": (oa, s2a, r2a, x2_s, x2_r), "b": (ob, s2b, r2b, y2_s, y2_r)}
    for piece in (2, 1, 3, 0):
        for colour in ("a", "b"):
            own, s2, r2, send, recv = seconds[colour]
            rcv = colours[colour][1]
            if piece in (1, 2):
                ring[colour, 9 if piece < 2 else 8].wait_recv()
            ring[colour, 4 + piece].wait_recv()
            total = own[piece] + rcv[8 + piece].astype(F32) + rcv[4 + piece].astype(F32)
            if piece == 0:
                own[0] = total
                continue
            s2[piece] = total.astype(BF16)
            to = device(y, xmod(piece), z, core) if colour == "a" else device(ymod(piece), x, z, core)
            copy = remote(s2.at[piece], r2.at[piece], send.at[piece], recv.at[piece], to)
            copy.start()
            sends.append(copy)
            second[colour, piece] = copy

    sums = []
    for colour, own, r2 in (("a", oa, r2a), ("b", ob, r2b)):
        total = own[0]
        for k in (1, 3, 2):
            second[colour, k].wait_recv()
            total = total + r2[k].astype(F32)
        sums.append(total)
    total = jnp.concatenate(sums, -1)

    spread_row = iota((NZ * 8, XB), 0)
    spread_of = lax.shift_right_logical(spread_row, 3) * OWN + jnp.bitwise_and(spread_row, 7)
    spread = (spread_of == iota((NZ * 8, XB), 1)) & (jnp.bitwise_and(spread_row, 7) < OWN)
    zs[...] = nn(spread.astype(F32).astype(BF16), total.astype(BF16)).reshape(NZ, 8, D).astype(BF16)
    last = []
    for k in (4, 3, 5, 2, 6, 1, 7):
        copy = remote(zs.at[k], zr.at[k], zz_s.at[k], zz_r.at[k], device(y, x, zmod(k), core))
        copy.start()
        sends.append(copy)
        last.append((k, copy))
    loss_copy.wait_recv()
    loss_ref[...] = (lsend[0:1, 0:1] + lrecv[0:1, 0:1]) * (1.0 / (2 * GROUP))
    final = total[0:OWN]
    for k, copy in reversed(last):
        copy.wait_recv()
        final = final + zr[k].astype(F32)[0:OWN]
    out_ref[...] = final
    for copy in sends:
        copy.wait_send()


def shards(q_hidden, p_hidden, w_up, w_down, pos_index, hard_index):
    vm = pltpu.VMEM
    dma = pltpu.SemaphoreType.DMA
    scratch = [
        pltpu.SMEM((1, 1), jnp.int32), pltpu.SMEM((1, 2), jnp.int32),
        vm((4 * LEN, D), BF16), vm((FF, D), BF16), vm((FF, D), BF16),
        vm((FF // 2, D), BF16), vm((FF // 2, D), BF16),
        vm((4 * LEN, D), BF16), vm((2, 8, 2 * LEN), F32), vm((FF // 2, 4 * LEN), F32), vm((FF // 2, 4 * LEN), F32),
        vm((NZ, 16, 128), BF16), vm((NZ * 16, 128), F32), vm((NY, 2, 2, 16, WIDE), BF16),
        vm((4, NX, XB, 4 * LEN), BF16),
        vm((NY, NX, XB, HALF), BF16), vm((NX, NY, XB, HALF), BF16),
        vm((NX, XB, HALF), F32), vm((NY, XB, HALF), F32),
        vm((12, XB, HALF), BF16), vm((12, XB, HALF), BF16),
        vm((4, XB, HALF), BF16), vm((4, XB, HALF), BF16),
        vm((4, XB, HALF), BF16), vm((4, XB, HALF), BF16), vm((4, XB, HALF), BF16), vm((4, XB, HALF), BF16),
        vm((NZ, 8, D), BF16), vm((NZ, 8, D), BF16), vm((8, 128), F32), vm((8, 128), F32),
        dma((7,)), dma((8,)), dma((8,)), dma((8,)), dma((8,)), dma((8,)), dma((8,)), dma((1,)), dma((1,)),
        dma((4,)), dma((4,)), dma((10,)), dma((10,)), dma((10,)), dma((10,)),
        dma((4,)), dma((4,)), dma((4,)), dma((4,)), dma((8,)), dma((8,)),
    ]
    hbm = pl.BlockSpec(memory_space=pltpu.HBM)
    out, loss = pl.pallas_call(
        kernel,
        out_shape=(pltpu.VMEM((OWN, D), F32), pltpu.VMEM((1, 1), F32)),
        in_specs=[hbm, hbm, hbm, hbm, hbm, hbm],
        out_specs=(pl.BlockSpec(memory_space=pltpu.VMEM), pl.BlockSpec(memory_space=pltpu.VMEM)),
        scratch_shapes=scratch,
        compiler_params=pltpu.CompilerParams(
            collective_id=0, has_side_effects=True, vmem_limit_bytes=VMEM_LIMIT
        ),
    )(pos_index, hard_index[0], q_hidden[0, 0], p_hidden[0, 0], w_up, w_down)
    return out, loss[0, 0]


def solution(mesh):
    return jax.shard_map(
        shards,
        mesh=mesh,
        in_specs=(
            P("rep", "dp", None, None),
            P("rep", "dp", None, None),
            P(),
            P(),
            P("rep", "dp"),
            P("rep", "dp", None),
        ),
        out_specs=(P(("dp", "rep"), None), P()),
        check_vma=False,
    )
```

time: 45.8 us -> 42.5 us (0.928)
  Pallas kernels: 42.7 us -> 39.4 us
    pallas_call x1, Pallas kernels: 42.7 us -> 39.4 us  [shards(): pl.pallas_call(kernel, out_shape=(pltpu.VMEM((OWN, D), F32), pltpu.VMEM((...]
where the time goes in v3:
time: 42.5 us; the launch traced here: 42.4 us
  Pallas kernels  39.4 us (93%)
  between operations  2.45 us (6%)
  local copies, waits for them, and re-layouts  0.61 us (1%)
    pallas_call x1, Pallas kernels, shards(): pl.pallas_call(kernel, out_shape=(pltpu.VMEM((OWN, D), F32), pltpu.VMEM((...  39.4 us

profile of v3, /device:TPU:1, one launch (start us, length us, event | category | flops | bytes accessed | tf_op | source)
XLA Modules:
  0.0 42.4 jit_solution(4977214199326401114)
XLA Ops:
  1.3 39.4 %shard_map.77 = (f32[6,768]{1,0:T(8,128)S(1)}, f32[1,1]{1,0:T(1,128)S(1)}) custom-call(s32[1,1]{1,0:T(1,128)S(6)} %copy.12.pos_hbm, s32[1,2]{1,0:T(1,128)} %bitcast.6, bf16[128,768]{1,0:T(8,128)(2,1)} %bitcast.4, bf16[128,768]{1,0:T(8,128)(2,1)} %bitcast.5, bf16[1536,768]{1,0:T(8,128)(2,1)} %wup_hbm.1, bf16[1536,768]{1,0:T(8,128)(2,1)} %wdn_hbm.1), custom_call_target="tpu_custom_call" | custom-call | tf_op jit(solution)/shard_map/pallas_call | solution.py:397
  40.7 0.6 %copy.10 = f32[6,768]{1,0:T(8,128)} copy(f32[6,768]{1,0:T(8,128)S(1)} %get-tuple-element.6) | data formatting | bytes 36864
